TPU v7x, 32 devices: a whole 2x2x4 slice. The times are simulated.
32 devices in a mesh: kv: 2 (over x), batch: 16 (over z, y, core).
Axes of the slice: x: 2, y: 2, z: 4, core: 2. Of those that a mesh axis runs over, the one named last changes fastest.
Arguments:
- queries: bfloat16 [64, 32, 128], P(('kv', 'batch')), may hold values from -64 to 64
- prefix_keys: bfloat16 [8192, 8, 128], P('batch', 'kv'), may hold values from -6 to 6
- prefix_values: bfloat16 [8192, 8, 128], P('batch', 'kv'), may hold values from -6 to 6
- suffix_keys: bfloat16 [64, 2048, 8, 128], P('batch', None, 'kv'), may hold values from -6 to 6
- suffix_values: bfloat16 [64, 2048, 8, 128], P('batch', None, 'kv'), may hold values from -6 to 6
- suffix_lengths: int32 [64], P('batch'), may hold values from 512 to 2048, as said below
- slot_sequence: int32 [64], P('batch'), may hold values from 0 to 63, as said below
Outputs:
- attended: bfloat16 [64, 32, 128], P(('kv', 'batch'))
Inputs may be any that keep to these rules, and one draw needn't show every extreme that they name: `suffix_lengths`: some slot holds exactly 2048 live tokens. `slot_sequence`: each sequence's suffix occupies exactly one slot; the 64 / 16 slots of one index of batch hold sequences whose output rows lie on pairwise different indices of batch.
All inputs are finite; a program needn't handle non-finite values.
Results may differ from a plain program's by a relative error of at most 0.007.
Values may be sent and summed in bfloat16 or wider, within the bound.
A program may use at most 64 MiB of HBM per device.

v0:
```python
import jax
import jax.numpy as jnp
from jax import lax
from jax.sharding import PartitionSpec as P

negative_fill = -1e30


def fold_block(state, keys_part, values_part, grouped, scale):
    best, total, accum = state
    scores = (
        jnp.einsum("rkjd,tkd->rkjt", grouped, keys_part, preferred_element_type=jnp.float32) * scale
    )
    new_best = jnp.maximum(best, jnp.max(scores, axis=-1))
    weights = jnp.exp(scores - new_best[..., None])
    total = jnp.sum(weights, axis=-1)
    accum = jnp.einsum(
        "rkjt,tkd->rkjd",
        weights.astype(jnp.bfloat16),
        values_part,
        preferred_element_type=jnp.float32,
    )
    return (new_best, total, accum)


def merge_rows(best, total, accum, row_ids, part_best, part_total, part_acc):
    old_best = best[row_ids]
    new_best = jnp.maximum(old_best, part_best)
    first = jnp.exp(old_best - new_best)
    second = jnp.exp(part_best - new_best)
    best = best.at[row_ids].set(new_best)
    total = total.at[row_ids].set(total[row_ids] * first + part_total * second)
    accum = accum.at[row_ids].set(accum[row_ids] * first[..., None] + part_acc * second[..., None])
    return (best, total, accum)


def shards(
    queries, prefix_keys, prefix_values, suffix_keys, suffix_values, suffix_lengths, slot_sequence
):
    kv_count = lax.axis_size("kv")
    batch_count = lax.axis_size("batch")
    per_device = queries.shape[0]
    head_count = queries.shape[1]
    head_dim = queries.shape[2]
    local_heads = head_count // kv_count
    kv_local = prefix_keys.shape[1]
    group_size = local_heads // kv_local
    scale = head_dim ** (-0.5)
    relayed = lax.all_to_all(queries, "kv", split_axis=1, concat_axis=0, tiled=True)
    gathered = lax.all_gather(relayed, "batch", axis=0, tiled=True)
    batch_total = gathered.shape[0]
    everyone = gathered.reshape(batch_count, kv_count, per_device, local_heads, head_dim)
    everyone = everyone.transpose(1, 0, 2, 3, 4).reshape(batch_total, local_heads, head_dim)
    slots = suffix_keys.shape[0]
    suffix_len = suffix_keys.shape[1]
    slot_queries = jnp.take(everyone, slot_sequence, axis=0).reshape(
        slots, kv_local, group_size, head_dim
    )
    scores = (
        jnp.einsum("skjd,stkd->skjt", slot_queries, suffix_keys, preferred_element_type=jnp.float32)
        * scale
    )
    position = jnp.arange(suffix_len)
    scores = jnp.where(
        position[None, None, None, :] < suffix_lengths[:, None, None, None], scores, negative_fill
    )
    suf_best = jnp.max(scores, axis=-1)
    weights = jnp.exp(scores - suf_best[..., None])
    suf_total = jnp.sum(weights, axis=-1)
    suf_acc = jnp.einsum(
        "skjt,stkd->skjd",
        weights.astype(jnp.bfloat16),
        suffix_values,
        preferred_element_type=jnp.float32,
    )
    grouped_all = everyone.reshape(batch_total, kv_local, group_size, head_dim)
    start_state = (
        jnp.full((batch_total, kv_local, group_size), negative_fill, jnp.float32),
        jnp.zeros((batch_total, kv_local, group_size), jnp.float32),
        jnp.zeros((batch_total, kv_local, group_size, head_dim), jnp.float32),
    )
    best, total, accum = fold_block(start_state, prefix_keys, prefix_values, grouped_all, scale)
    best, total, accum = merge_rows(best, total, accum, slot_sequence, suf_best, suf_total, suf_acc)
    got_acc, got_best, got_total = (
        lax.all_to_all(
            lax.all_to_all(
                accum.reshape(batch_total, 1, local_heads, head_dim),
                "kv",
                split_axis=0,
                concat_axis=2,
                tiled=True,
            ),
            "batch",
            split_axis=0,
            concat_axis=1,
            tiled=True,
        ),
        lax.all_to_all(
            lax.all_to_all(
                best.reshape(batch_total, 1, local_heads),
                "kv",
                split_axis=0,
                concat_axis=2,
                tiled=True,
            ),
            "batch",
            split_axis=0,
            concat_axis=1,
            tiled=True,
        ),
        lax.all_to_all(
            lax.all_to_all(
                total.reshape(batch_total, 1, local_heads),
                "kv",
                split_axis=0,
                concat_axis=2,
                tiled=True,
            ),
            "batch",
            split_axis=0,
            concat_axis=1,
            tiled=True,
        ),
    )
    top = jnp.max(got_best, axis=1)
    factor = jnp.exp(got_best - top[:, None, :])
    denominator = jnp.sum(got_total * factor, axis=1)
    numerator = jnp.sum(got_acc * factor[..., None], axis=1)
    return (numerator / denominator[..., None]).astype(jnp.bfloat16)


def solution(mesh):
    return jax.shard_map(
        shards,
        mesh=mesh,
        in_specs=(
            P(("kv", "batch"), None, None),
            P("batch", "kv", None),
            P("batch", "kv", None),
            P("batch", None, "kv", None),
            P("batch", None, "kv", None),
            P("batch"),
            P("batch"),
        ),
        out_specs=P(("kv", "batch"), None, None),
        check_vma=False,
    )
```

profile of v0, /device:TPU:0, one launch (start us, length us, event | category | flops | bytes accessed | tf_op | source)
XLA Modules:
  0.0 114.2 jit_solution(14936565666871693103)
XLA Ops:
  0.0 1.4 %copy.73 = bf16[2,32,128]{2,0,1:T(2,128)(2,1)} copy(bf16[2,32,128]{2,1,0:T(8,128)(2,1)} %param.7) | data formatting | bytes 32768 | tf_op args[0]
  1.4 4.2 %all-to-all-start = ((bf16[2,32,128]{2,0,1:T(2,128)(2,1)}), bf16[2,32,128]{2,0,1:T(2,128)(2,1)S(1)}, u32[]{:S(2)}, u32[]{:S(2)}) async-start(bf16[2,32,128]{2,0,1:T(2,128)(2,1)} %copy.73), calls=%async_computation | async-start | bytes 32768 | tf_op jit(solution)/shard_map/all_to_all | solution.py:49
  7.0 0.7 iota_compare_fusion
  7.7 1.8 %all-to-all-done = bf16[2,32,128]{2,0,1:T(2,128)(2,1)S(1)} async-done(((bf16[2,32,128]{2,0,1:T(2,128)(2,1)}), bf16[2,32,128]{2,0,1:T(2,128)(2,1)S(1)}, u32[]{:S(2)}, u32[]{:S(2)}) %all-to-all-start) | async-done | bytes 16416 | tf_op jit(solution)/shard_map/all_to_all | solution.py:49
  9.5 22.8 %all_gather.3 = bf16[64,16,128]{2,1,0:T(8,128)(2,1)S(1)} all-gather(bf16[4,16,128]{2,1,0:T(8,128)(2,1)S(1)} %bitcast.81), channel_id=1, replica_groups=mesh['kv'=2,'batch'=16] {'batch'}, dimensions={0}, use_global_device_ids=true | all-gather | bytes 278528 | tf_op jit(solution)/shard_map/all_gather | solution.py:50
  32.6 1.6 %bitcast_reduce_fusion = (f32[64,4,4]{0,2,1:T(4,128)S(1)}, f32[4,512,64,4]{1,2,3,0:T(8,128)S(1)}) fusion(bf16[64,4,4,128]{3,0,2,1:T(8,128)(2,1)S(1)} %bitcast.73, bf16[512,4,128,1]{2,1,0,3:T(4,128)(2,1)} %bitcast.74), kind=kOutput, calls=%fused_computation.14 | convolution fusion | flops 135265280 | bytes 2887680 | tf_op jit(solution)/shard_map/rkjd,tkd->rkjt/dot_general | solution.py:12
  36.8 5.8 %fusion.34 = (f32[4,4,4]{2,1,0:T(4,128)S(1)}, f32[4,4,4,2048]{3,2,1,0:T(4,128)S(1)}) fusion(bf16[4,2048,4,128]{3,2,1,0:T(4,128)(2,1)} %param.10, bf16[4,4,4,128]{3,2,1,0:T(4,128)(2,1)S(1)} %bitcast.95, pred[4]{0:T(512)(128)(4,1)S(1)} %compare_and_fusion, pred[4,2048]{1,0:T(4,128)(4,1)S(1)} %iota_compare_fusion), kind=kOutput, calls=%fused_computation.47 | convolution fusion | flops 33955776 | bytes 8937732 | tf_op jit(solution)/shard_map/skjd,stkd->skjt/dot_general | solution.py:60
  45.5 3.2 %all-to-all-start.5 = ((f32[2,1,512]{2,1,0:T(1,128)}), f32[2,1,512]{2,1,0:T(1,128)S(1)}, u32[]{:S(2)}, u32[]{:S(2)}) async-start(f32[2,1,512]{2,1,0:T(1,128)} %reshape.140), calls=%async_computation.5 | async-start | bytes 8192 | tf_op jit(solution)/shard_map/all_to_all | solution.py:112
  50.8 1.7 %all-to-all-done.5 = f32[2,1,512]{2,1,0:T(1,128)S(1)} async-done(((f32[2,1,512]{2,1,0:T(1,128)}), f32[2,1,512]{2,1,0:T(1,128)S(1)}, u32[]{:S(2)}, u32[]{:S(2)}) %all-to-all-start.5) | async-done | bytes 4128 | tf_op jit(solution)/shard_map/all_to_all | solution.py:112
  52.5 3.2 %all-to-all-start.3 = ((f32[2,1,512]{2,1,0:T(1,128)}), f32[2,1,512]{2,1,0:T(1,128)S(1)}, u32[]{:S(2)}, u32[]{:S(2)}) async-start(f32[2,1,512]{2,1,0:T(1,128)} %reshape.138), calls=%async_computation.3 | async-start | bytes 8192 | tf_op jit(solution)/shard_map/all_to_all | solution.py:99
  56.3 1.1 copy.84
  57.5 1.6 %gather_fusion = f32[4,4,4,128]{3,2,1,0:T(4,128)S(1)} fusion(f32[64,4,4,128]{3,2,1,0:T(4,128)} %copy.84, s32[1024]{0:T(1024)S(1)} %pad_clamp_fusion), kind=kCustom, calls=%fused_computation | custom fusion | bytes 65552 | tf_op jit(solution)/shard_map/gather | solution.py:33
  59.9 0.7 copy.100
  60.6 3.5 %all-to-all-start.6 = ((f32[32,1,32]{2,1,0:T(1,128)}), f32[32,1,32]{2,1,0:T(1,128)S(1)}, u32[]{:S(2)}, u32[]{:S(2)}) async-start(f32[32,1,32]{2,1,0:T(1,128)} %copy.100), calls=%async_computation.6 | async-start | bytes 32768 | tf_op jit(solution)/shard_map/all_to_all | solution.py:111
  64.1 4.7 %fusion.16 = f32[4,4,4,128]{3,2,1,0:T(4,128)S(1)} fusion(bf16[4,2048,4,128]{3,2,1,0:T(4,128)(2,1)} %param.11, f32[4,4,4,2048]{3,2,1,0:T(4,128)S(1)} %get-tuple-element.14, f32[4,4,4]{2,1,0:T(4,128)S(1)} %get-tuple-element.13, f32[4,4,4,128]{3,2,1,0:T(4,128)S(1)} %gather_fusion, f32[4,4,4]{2,1,0:T(4,128)S(1)} %bitcast.97, f32[4,4,4]{2,1,0:T(4,128)S(1)} %bitcast.96), kind=kOutput, calls=%fused_computation.20 | convolution fusion | flops 33841152 | bytes 8979200 | tf_op jit(solution)/shard_map/skjt,stkd->skjd/dot_general | solution.py:70
  68.8 1.9 %scatter_fusion = f32[64,4,4,128]{3,2,1,0:T(4,128)} fusion(f32[64,4,4,128]{3,2,1,0:T(4,128)} %copy.84, s32[4]{0:T(128)S(1)} %compare_select_fusion, f32[4,4,4,128]{3,2,1,0:T(4,128)S(1)} %fusion.16), kind=kCustom, calls=%fused_computation.4 | custom fusion | bytes 98320 | tf_op jit(solution)/shard_map/scatter | solution.py:33
  70.7 3.5 %all-to-all-start.1 = ((f32[64,1,16,128]{3,2,1,0:T(8,128)}), f32[64,1,16,128]{3,2,1,0:T(8,128)S(1)}, u32[]{:S(2)}, u32[]{:S(2)}) async-start(f32[64,1,16,128]{3,2,1,0:T(8,128)} %bitcast.14), calls=%async_computation.1 | async-start | bytes 1048576 | tf_op jit(solution)/shard_map/all_to_all | solution.py:86
  75.7 7.5 %all-to-all-done.1 = f32[64,1,16,128]{3,2,1,0:T(8,128)S(1)} async-done(((f32[64,1,16,128]{3,2,1,0:T(8,128)}), f32[64,1,16,128]{3,2,1,0:T(8,128)S(1)}, u32[]{:S(2)}, u32[]{:S(2)}) %all-to-all-start.1) | async-done | bytes 524320 | tf_op jit(solution)/shard_map/all_to_all | solution.py:86
  83.2 5.8 %all-to-all-start.4 = ((f32[32,1,32]{2,1,0:T(1,128)}), f32[32,1,32]{2,1,0:T(1,128)S(1)}, u32[]{:S(2)}, u32[]{:S(2)}) async-start(f32[32,1,32]{2,1,0:T(1,128)} %copy.93), calls=%async_computation.4 | async-start | bytes 32768 | tf_op jit(solution)/shard_map/all_to_all | solution.py:98
  89.0 0.9 copy.86
  89.8 5.6 %all-to-all-done.4 = f32[32,1,32]{2,1,0:T(1,128)S(1)} async-done(((f32[32,1,32]{2,1,0:T(1,128)}), f32[32,1,32]{2,1,0:T(1,128)S(1)}, u32[]{:S(2)}, u32[]{:S(2)}) %all-to-all-start.4) | async-done | bytes 4128 | tf_op jit(solution)/shard_map/all_to_all | solution.py:98
  95.5 3.6 %all-to-all-start.2 = ((f32[32,1,32,128]{3,2,1,0:T(8,128)}), f32[32,1,32,128]{3,2,1,0:T(8,128)S(1)}, u32[]{:S(2)}, u32[]{:S(2)}) async-start(f32[32,1,32,128]{3,2,1,0:T(8,128)} %bitcast.18), calls=%async_computation.2 | async-start | bytes 1048576 | tf_op jit(solution)/shard_map/all_to_all | solution.py:85
  99.1 14.2 %all-to-all-done.2 = f32[32,1,32,128]{3,2,1,0:T(8,128)S(1)} async-done(((f32[32,1,32,128]{3,2,1,0:T(8,128)}), f32[32,1,32,128]{3,2,1,0:T(8,128)S(1)}, u32[]{:S(2)}, u32[]{:S(2)}) %all-to-all-start.2) | async-done | bytes 524320 | tf_op jit(solution)/shard_map/all_to_all | solution.py:85
  113.5 0.7 divide_convert_fusion
  (44 shorter events, 12.3 us)
Async XLA Ops:
  0.0 55.7 %copy-start = (bf16[512,4,128]{2,1,0:T(4,128)(2,1)S(1)}, bf16[512,4,128]{2,1,0:T(4,128)(2,1)}, u32[]{:S(2)}) copy-start(bf16[512,4,128]{2,1,0:T(4,128)(2,1)} %param.9) | copy-start | bytes 1572868
  1.4 8.1 %all-to-all-start = ((bf16[2,32,128]{2,0,1:T(2,128)(2,1)}), bf16[2,32,128]{2,0,1:T(2,128)(2,1)S(1)}, u32[]{:S(2)}, u32[]{:S(2)}) async-start(bf16[2,32,128]{2,0,1:T(2,128)(2,1)} %copy.73), calls=%async_computation | async-start | bytes 32768 | tf_op jit(solution)/shard_map/all_to_all | solution.py:49
  45.5 7.0 %all-to-all-start.5 = ((f32[2,1,512]{2,1,0:T(1,128)}), f32[2,1,512]{2,1,0:T(1,128)S(1)}, u32[]{:S(2)}, u32[]{:S(2)}) async-start(f32[2,1,512]{2,1,0:T(1,128)} %reshape.140), calls=%async_computation.5 | async-start | bytes 8192 | tf_op jit(solution)/shard_map/all_to_all | solution.py:112
  52.5 8.0 %all-to-all-start.3 = ((f32[2,1,512]{2,1,0:T(1,128)}), f32[2,1,512]{2,1,0:T(1,128)S(1)}, u32[]{:S(2)}, u32[]{:S(2)}) async-start(f32[2,1,512]{2,1,0:T(1,128)} %reshape.138), calls=%async_computation.3 | async-start | bytes 8192 | tf_op jit(solution)/shard_map/all_to_all | solution.py:99
  60.6 10.2 %all-to-all-start.6 = ((f32[32,1,32]{2,1,0:T(1,128)}), f32[32,1,32]{2,1,0:T(1,128)S(1)}, u32[]{:S(2)}, u32[]{:S(2)}) async-start(f32[32,1,32]{2,1,0:T(1,128)} %copy.100), calls=%async_computation.6 | async-start | bytes 32768 | tf_op jit(solution)/shard_map/all_to_all | solution.py:111
  70.7 12.4 %all-to-all-start.1 = ((f32[64,1,16,128]{3,2,1,0:T(8,128)}), f32[64,1,16,128]{3,2,1,0:T(8,128)S(1)}, u32[]{:S(2)}, u32[]{:S(2)}) async-start(f32[64,1,16,128]{3,2,1,0:T(8,128)} %bitcast.14), calls=%async_computation.1 | async-start | bytes 1048576 | tf_op jit(solution)/shard_map/all_to_all | solution.py:86
  83.2 12.3 %all-to-all-start.4 = ((f32[32,1,32]{2,1,0:T(1,128)}), f32[32,1,32]{2,1,0:T(1,128)S(1)}, u32[]{:S(2)}, u32[]{:S(2)}) async-start(f32[32,1,32]{2,1,0:T(1,128)} %copy.93), calls=%async_computation.4 | async-start | bytes 32768 | tf_op jit(solution)/shard_map/all_to_all | solution.py:98
  95.5 17.8 %all-to-all-start.2 = ((f32[32,1,32,128]{3,2,1,0:T(8,128)}), f32[32,1,32,128]{3,2,1,0:T(8,128)S(1)}, u32[]{:S(2)}, u32[]{:S(2)}) async-start(f32[32,1,32,128]{3,2,1,0:T(8,128)} %bitcast.18), calls=%async_computation.2 | async-start | bytes 1048576 | tf_op jit(solution)/shard_map/all_to_all | solution.py:85
where the time goes:
time: 115 us; the launch traced here: 114 us
  waiting for transfers between devices  30.7 us (27%)
  starting transfers between devices  27.1 us (24%)
  blocking collectives  22.8 us (20%)
  local copies, waits for them, and re-layouts  14.4 us (13%)
  matrix products  12.6 us (11%)
  other arithmetic  6.31 us (5%)
    all_gather x1, blocking collectives, shards(): gathered = lax.all_gather(relayed, 'batch', axis=0, tiled=True)  22.8 us
    all_to_all x1, waiting for transfers between devices, shards(): lax.all_to_all(lax.all_to_all(accum.reshape(batch_total, 1, local_heads,...  14.2 us
    all_to_all x1, waiting for transfers between devices, shards(): lax.all_to_all(accum.reshape(batch_total, 1, local_heads, head_dim), 'kv'...  7.45 us
    all_to_all x1, starting transfers between devices, shards(): lax.all_to_all(lax.all_to_all(best.reshape(batch_total, 1, local_heads),...  5.82 us
    dot_general x1, matrix products, shards(): jnp.einsum('skjd,stkd->skjt', slot_queries, suffix_keys, preferred_elemen...  5.77 us
    all_to_all x1, waiting for transfers between devices, shards(): lax.all_to_all(lax.all_to_all(best.reshape(batch_total, 1, local_heads),...  5.64 us
    dot_general x1, matrix products, shards(): jnp.einsum('skjt,stkd->skjd', weights.astype(jnp.bfloat16), suffix_values...  4.73 us
    all_to_all x1, starting transfers between devices, shards(): lax.all_to_all(queries, 'kv', split_axis=1, concat_axis=0, tiled=True)  4.23 us
  transfers between devices with their start and end apart: 7, of which 5 were waited for; matrix products, arithmetic and copies ran while one was open for 16% of the time, Pallas kernels for 0%

commit v1 on v0

v1 whole, which is shorter than its diff:
```python
import functools

import jax
import jax.numpy as jnp
from jax import lax
from jax.experimental import pallas as pl
from jax.experimental.pallas import tpu as pltpu
from jax.sharding import PartitionSpec as P

MESH = pl.DeviceIdType.MESH
FILL = -1e30
F32 = jnp.float32
BF16 = jnp.bfloat16


def kernel(
    kv_count,
    batch_count,
    group,
    scale,
    seq_ref,
    len_ref,
    q_ref,
    pk_hbm,
    pv_hbm,
    sk_hbm,
    sv_hbm,
    out_ref,
    pk_raw,
    pv_raw,
    sk,
    sv,
    spread,
    pk,
    pv,
    qbuf,
    qf,
    acc,
    best,
    total,
    suf_acc,
    suf_best,
    suf_total,
    send_acc,
    send_stat,
    recv_acc,
    recv_stat,
    weight,
    pre_sem,
    suf_sem,
    q_send,
    q_recv,
    a_send,
    a_recv,
    s_send,
    s_recv,
):
    devices = kv_count * batch_count
    per_device, heads, dim = q_ref.shape
    local = heads // kv_count
    kv_local = local // group
    sequences = devices * per_device
    slots, rows, _ = sk_hbm.shape
    prefix_rows = pk_hbm.shape[0]
    prefix = prefix_rows // kv_local

    my_kv = lax.axis_index("kv")
    my_batch = lax.axis_index("batch")
    me = my_kv * batch_count + my_batch

    pre_copies = [
        pltpu.make_async_copy(pk_hbm, pk_raw, pre_sem.at[0]),
        pltpu.make_async_copy(pv_hbm, pv_raw, pre_sem.at[1]),
    ]
    for copy in pre_copies:
        copy.start()

    def suffix_copies(slot):
        return (
            pltpu.make_async_copy(sk_hbm.at[slot], sk.at[slot], suf_sem.at[0, slot]),
            pltpu.make_async_copy(sv_hbm.at[slot], sv.at[slot], suf_sem.at[1, slot]),
        )

    for slot in range(slots):
        for copy in suffix_copies(slot):
            copy.start()

    barrier = pltpu.get_barrier_semaphore()

    def peer(step):
        other = lax.rem(me + step, devices)
        return other, (other // batch_count, lax.rem(other, batch_count))

    def greet(step, carry):
        _, place = peer(step)
        pl.semaphore_signal(barrier, inc=1, device_id=place, device_id_type=MESH)
        return carry

    lax.fori_loop(1, devices, greet, 0)
    pl.semaphore_wait(barrier, devices - 1)

    def query_copy(step):
        other, place = peer(step)
        heads_there = pl.ds(pl.multiple_of(place[0] * local, local), local)
        return pltpu.make_async_remote_copy(
            src_ref=q_ref.at[:, heads_there, :],
            dst_ref=qbuf.at[pl.ds(me * per_device, per_device)],
            send_sem=q_send.at[other],
            recv_sem=q_recv.at[me],
            device_id=place,
            device_id_type=MESH,
        )

    def query_arrival(step):
        other, place = peer(step)
        return pltpu.make_async_remote_copy(
            src_ref=q_ref.at[:, pl.ds(0, local), :],
            dst_ref=qbuf.at[pl.ds(other * per_device, per_device)],
            send_sem=q_send.at[other],
            recv_sem=q_recv.at[other],
            device_id=place,
            device_id_type=MESH,
        )

    def query_start(step, carry):
        query_copy(step).start()
        return carry

    lax.fori_loop(1, devices, query_start, 0)
    my_heads = pl.ds(pl.multiple_of(my_kv * local, local), local)
    qbuf[pl.ds(me * per_device, per_device)] = q_ref[:, my_heads, :]

    for copy, raw, parted in zip(pre_copies, (pk_raw, pv_raw), (pk, pv)):
        copy.wait()
        spread[...] = raw[...].astype(F32)
        for k in range(kv_local):
            parted[k] = spread[pl.ds(k, prefix, stride=kv_local), :].astype(BF16)

    def query_wait(step, carry):
        query_arrival(step).wait()
        return carry

    lax.fori_loop(1, devices, query_wait, 0)

    qf[...] = qbuf[...].astype(F32).reshape(sequences * local, dim)
    contract_last = (((1,), (1,)), ((), ()))
    for k in range(kv_local):
        parts = [qf[pl.ds(k * group + j, sequences, stride=local), :] for j in range(group)]
        q = jnp.concatenate(parts, axis=0).astype(BF16)
        scores = lax.dot_general(q, pk[k], contract_last, preferred_element_type=F32) * scale
        row_best = jnp.max(scores, axis=-1, keepdims=True)
        weights = jnp.exp(scores - row_best)
        row_total = jnp.sum(weights, axis=-1, keepdims=True)
        row_acc = jnp.dot(weights.astype(BF16), pv[k], preferred_element_type=F32)
        wide_best = jnp.broadcast_to(row_best, row_acc.shape)
        wide_total = jnp.broadcast_to(row_total, row_acc.shape)
        for j in range(group):
            there = pl.ds(k * group + j, sequences, stride=local)
            here = slice(j * sequences, (j + 1) * sequences)
            acc[there, :] = row_acc[here]
            best[there, :] = wide_best[here]
            total[there, :] = wide_total[here]

    column = lax.broadcasted_iota(jnp.int32, (local, rows), 1)
    head_row = lax.broadcasted_iota(jnp.int32, (local, rows), 0)
    own_head = lax.rem(column, kv_local) == head_row // group
    for slot in range(slots):
        for copy in suffix_copies(slot):
            copy.wait()
        q = qbuf[seq_ref[slot]]
        scores = lax.dot_general(q, sk[slot], contract_last, preferred_element_type=F32) * scale
        live = own_head & (column < len_ref[slot] * kv_local)
        scores = jnp.where(live, scores, FILL)
        row_best = jnp.max(scores, axis=-1, keepdims=True)
        weights = jnp.exp(scores - row_best)
        row_total = jnp.sum(weights, axis=-1, keepdims=True)
        suf_acc[slot] = jnp.dot(weights.astype(BF16), sv[slot], preferred_element_type=F32)
        suf_best[slot] = jnp.broadcast_to(row_best, (local, dim))
        suf_total[slot] = jnp.broadcast_to(row_total, (local, dim))

    lane = lax.broadcasted_iota(jnp.int32, (local, dim), 1)
    sub = lax.broadcasted_iota(jnp.int32, (local, dim), 0)
    half = per_device * local

    def merged(other):
        accs = []
        stat = jnp.zeros((local, dim), F32)
        for w in range(per_device):
            sequence = other * per_device + w
            at = jnp.int32(0)
            hit = jnp.int32(0)
            for slot in range(slots):
                same = (seq_ref[slot] == sequence).astype(jnp.int32)
                at = jnp.maximum(at, same * slot)
                hit = jnp.maximum(hit, same)
            table = pl.ds(pl.multiple_of(sequence * local, local), local)
            first_best = best[table, :]
            second_best = jnp.where(hit > 0, suf_best[at], FILL)
            new_best = jnp.maximum(first_best, second_best)
            first = jnp.exp(first_best - new_best)
            second = jnp.where(hit > 0, jnp.exp(second_best - new_best), 0.0)
            new_total = total[table, :] * first + suf_total[at] * second
            accs.append((acc[table, :] * first + suf_acc[at] * second).astype(BF16))
            stat = jnp.where(lane == sub + w * local, new_best, stat)
            stat = jnp.where(lane == sub + half + w * local, new_total, stat)
        return accs, jnp.sum(stat, axis=0, keepdims=True)

    def result_copies(step):
        other, place = peer(step)
        return (
            pltpu.make_async_remote_copy(
                src_ref=send_acc.at[other],
                dst_ref=recv_acc.at[me],
                send_sem=a_send.at[other],
                recv_sem=a_recv.at[me],
                device_id=place,
                device_id_type=MESH,
            ),
            pltpu.make_async_remote_copy(
                src_ref=send_stat.at[other],
                dst_ref=recv_stat.at[me],
                send_sem=s_send.at[other],
                recv_sem=s_recv.at[me],
                device_id=place,
                device_id_type=MESH,
            ),
        )

    def result_arrivals(step):
        other, place = peer(step)
        return (
            pltpu.make_async_remote_copy(
                src_ref=send_acc.at[other],
                dst_ref=recv_acc.at[other],
                send_sem=a_send.at[other],
                recv_sem=a_recv.at[other],
                device_id=place,
                device_id_type=MESH,
            ),
            pltpu.make_async_remote_copy(
                src_ref=send_stat.at[other],
                dst_ref=recv_stat.at[other],
                send_sem=s_send.at[other],
                recv_sem=s_recv.at[other],
                device_id=place,
                device_id_type=MESH,
            ),
        )

    def result_start(step, carry):
        other, _ = peer(step)
        accs, stat = merged(other)
        for w in range(per_device):
            send_acc[other, w] = accs[w]
        send_stat[other] = stat
        for copy in result_copies(step):
            copy.start()
        return carry

    lax.fori_loop(1, devices, result_start, 0)
    accs, stat = merged(me)
    for w in range(per_device):
        recv_acc[me, w] = accs[w]
    recv_stat[me] = stat

    def result_wait(step, carry):
        for copy in result_arrivals(step):
            copy.wait()
        return carry

    lax.fori_loop(1, devices, result_wait, 0)

    for g in range(kv_count):
        own = slice(g * batch_count, (g + 1) * batch_count)
        stats = recv_stat[own, 0, :]
        part_best = stats[:, :half]
        part_total = stats[:, half : 2 * half]
        top = jnp.max(part_best, axis=0, keepdims=True)
        factor = jnp.exp(part_best - top)
        denominator = jnp.sum(part_total * factor, axis=0, keepdims=True)
        weight[own, 0, :] = jnp.concatenate(
            [factor / denominator, jnp.zeros((batch_count, dim - half), F32)], axis=1
        )

        def add(index, sums):
            source = g * batch_count + index
            row = weight[source]
            new = []
            for w in range(per_device):
                picked = jnp.where(lane == sub + w * local, row, 0.0)
                share = jnp.sum(picked, axis=-1, keepdims=True)
                new.append(sums[w] + share * recv_acc[source, w].astype(F32))
            return tuple(new)

        start = tuple(jnp.zeros((local, dim), F32) for _ in range(per_device))
        sums = lax.fori_loop(0, batch_count, add, start, unroll=4)
        for w in range(per_device):
            out_ref[w, g * local : (g + 1) * local, :] = sums[w].astype(BF16)


def solution(mesh):
    kv_count = mesh.shape["kv"]
    batch_count = mesh.shape["batch"]
    devices = kv_count * batch_count

    def step(queries, prefix_keys, prefix_values, suffix_keys, suffix_values, lengths, slot_sequence):
        per_device, heads, dim = queries.shape
        local = heads // kv_count
        prefix, kv_local, _ = prefix_keys.shape
        slots, suffix, _, _ = suffix_keys.shape
        group = local // kv_local
        sequences = devices * per_device
        flat = sequences * local
        vmem = pl.BlockSpec(memory_space=pltpu.VMEM)
        smem = pl.BlockSpec(memory_space=pltpu.SMEM)
        hbm = pl.BlockSpec(memory_space=pl.ANY)
        dma = pltpu.SemaphoreType.DMA
        return pl.pallas_call(
            functools.partial(kernel, kv_count, batch_count, group, dim ** (-0.5)),
            out_shape=jax.ShapeDtypeStruct(queries.shape, BF16),
            in_specs=[smem, smem, vmem, hbm, hbm, hbm, hbm],
            out_specs=vmem,
            scratch_shapes=[
                pltpu.VMEM((prefix * kv_local, dim), BF16),
                pltpu.VMEM((prefix * kv_local, dim), BF16),
                pltpu.VMEM((slots, suffix * kv_local, dim), BF16),
                pltpu.VMEM((slots, suffix * kv_local, dim), BF16),
                pltpu.VMEM((prefix * kv_local, dim), F32),
                pltpu.VMEM((kv_local, prefix, dim), BF16),
                pltpu.VMEM((kv_local, prefix, dim), BF16),
                pltpu.VMEM((sequences, local, dim), BF16),
                pltpu.VMEM((flat, dim), F32),
                pltpu.VMEM((flat, dim), F32),
                pltpu.VMEM((flat, dim), F32),
                pltpu.VMEM((flat, dim), F32),
                pltpu.VMEM((slots, local, dim), F32),
                pltpu.VMEM((slots, local, dim), F32),
                pltpu.VMEM((slots, local, dim), F32),
                pltpu.VMEM((devices, per_device, local, dim), BF16),
                pltpu.VMEM((devices, 1, dim), F32),
                pltpu.VMEM((devices, per_device, local, dim), BF16),
                pltpu.VMEM((devices, 1, dim), F32),
                pltpu.VMEM((devices, 1, dim), F32),
                dma((2,)),
                dma((2, slots)),
                dma((devices,)),
                dma((devices,)),
                dma((devices,)),
                dma((devices,)),
                dma((devices,)),
                dma((devices,)),
            ],
            compiler_params=pltpu.CompilerParams(
                collective_id=0, has_side_effects=True, vmem_limit_bytes=60 * 1024 * 1024
            ),
        )(
            slot_sequence,
            lengths,
            queries,
            prefix_keys.reshape(prefix * kv_local, dim),
            prefix_values.reshape(prefix * kv_local, dim),
            suffix_keys.reshape(slots, suffix * kv_local, dim),
            suffix_values.reshape(slots, suffix * kv_local, dim),
        )

    return jax.shard_map(
        step,
        mesh=mesh,
        in_specs=(
            P(("kv", "batch"), None, None),
            P("batch", "kv", None),
            P("batch", "kv", None),
            P("batch", None, "kv", None),
            P("batch", None, "kv", None),
            P("batch"),
            P("batch"),
        ),
        out_specs=P(("kv", "batch"), None, None),
        check_vma=False,
    )
```

time: 115 us -> 35.5 us (0.31)
  Pallas kernels: 0 us -> 33.8 us
  waiting for transfers between devices: 30.7 us -> 0 us
  starting transfers between devices: 27.1 us -> 0 us
  blocking collectives: 22.8 us -> 0 us
  local copies, waits for them, and re-layouts: 14.4 us -> 1.32 us
  matrix products: 12.6 us -> 0 us
  other arithmetic: 6.31 us -> 0 us
    pallas_call x0 -> x1, Pallas kernels: none -> 33.8 us  [step(): pl.pallas_call(functools.partial(kernel, kv_count, batch_count, group, di...]
    all_to_all x7 -> x0, waiting for transfers between devices: 30.7 us -> none  [the longest x1 14.2 us: shards(): lax.all_to_all(lax.all_to_all(accum.reshape(batch_total, 1, local_heads,...]
    all_to_all x7 -> x0, starting transfers between devices: 27.1 us -> none  [the longest x1 5.82 us: shards(): lax.all_to_all(lax.all_to_all(best.reshape(batch_total, 1, local_heads),...]
    all_gather x1 -> x0, blocking collectives: 22.8 us -> none  [shards(): gathered = lax.all_gather(relayed, 'batch', axis=0, tiled=True)]
    dot_general x4 -> x0, matrix products: 12.6 us -> none  [the longest x1 5.77 us: shards(): jnp.einsum('skjd,stkd->skjt', slot_queries, suffix_keys, preferred_elemen...]
    scatter x5 -> x0, local copies, waits for them, and re-layouts: 3.39 us -> none  [the longest x1 1.93 us: merge_rows(): accum.at[row_ids]]
    gather x4 -> x0, local copies, waits for them, and re-layouts: 3.32 us -> none  [the longest x1 1.62 us: merge_rows(): accum[row_ids] * first[..., None] + part_acc * second[..., None]]
    all_to_all x9 -> x0, local copies, waits for them, and re-layouts: 2.4 us -> none  [the longest x1 0.86 us: shards(): lax.all_to_all(accum.reshape(batch_total, 1, local_heads, head_dim), 'kv'...]
  transfers between devices with their start and end apart: 7 -> 0, of which waited for: 5 -> 0; matrix products, arithmetic and copies ran while one was open for 16% -> 0% of each run, Pallas kernels for 0% -> 0%
where the time goes in v1:
time: 35.5 us; the launch traced here: 35.2 us
  Pallas kernels  33.8 us (95%)
  local copies, waits for them, and re-layouts  1.32 us (4%)
    pallas_call x1, Pallas kernels, step(): pl.pallas_call(functools.partial(kernel, kv_count, batch_count, group, di...  33.8 us
    unnamed x1, local copies, waits for them, and re-layouts  1.32 us

profile of v1, /device:TPU:0, one launch (start us, length us, event | category | flops | bytes accessed | tf_op | source)
XLA Modules:
  0.0 35.2 jit_solution(18334334638686419030)
XLA Ops:
  0.0 33.8 %shard_map.73 = bf16[2,32,128]{2,1,0:T(8,128)(2,1)} custom-call(s32[4]{0:T(128)} %seq_ref.1, s32[4]{0:T(128)} %len_ref.1, bf16[2,32,128]{2,1,0:T(8,128)(2,1)} %q_ref.1, bf16[2048,128]{1,0:T(8,128)(2,1)} %bitcast.6, bf16[2048,128]{1,0:T(8,128)(2,1)} %bitcast.7, bf16[4,8192,128]{2,1,0:T(8,128)(2,1)} %bitcast.4, bf16[4,8192,128]{2,1,0:T(8,128)(2,1)} %bitcast.5), custom_call_target="tpu_custom_call" | custom-call | tf_op jit(solution)/shard_map/pallas_call | solution.py:318
  33.9 1.3 %copy.9 = bf16[2,32,128]{2,1,0:T(8,128)(2,1)} copy(bf16[2,32,128]{2,1,0:T(8,128)(2,1)} %shard_map.73) | data formatting | bytes 32768

commit v2 on v1

v2 whole, which is shorter than its diff:
```python
import functools

import jax
import jax.numpy as jnp
from jax import lax
from jax.experimental import pallas as pl
from jax.experimental.pallas import tpu as pltpu
from jax.sharding import PartitionSpec as P

MESH = pl.DeviceIdType.MESH
FILL = -1e30
F32 = jnp.float32
BF16 = jnp.bfloat16


def kernel(
    kv_count,
    batch_count,
    group,
    scale,
    seq_ref,
    len_ref,
    q_ref,
    pk_hbm,
    pv_hbm,
    sk_hbm,
    sv_hbm,
    out_ref,
    pk_raw,
    pv_raw,
    sk,
    sv,
    spread,
    pk,
    pv,
    qbuf,
    qf,
    acc,
    best,
    total,
    mate_acc,
    mate_best,
    mate_total,
    suf_acc,
    suf_best,
    suf_total,
    send_acc,
    send_stat,
    recv_acc,
    recv_stat,
    send_suf,
    send_sufstat,
    recv_suf,
    recv_sufstat,
    weight,
    pre_sem,
    suf_sem,
    q_send,
    q_recv,
    f_send,
    f_recv,
    m_send,
    m_recv,
    r_send,
    r_recv,
    u_send,
    u_recv,
):
    devices = kv_count * batch_count
    per_device, heads, dim = q_ref.shape
    local = heads // kv_count
    kv_local = local // group
    slots, rows, _ = sk_hbm.shape
    prefix_rows = pk_hbm.shape[0]
    prefix = prefix_rows // kv_local

    my_kv = lax.axis_index("kv")
    my_batch = lax.axis_index("batch")
    me = my_kv * batch_count + my_batch
    pairs = devices // 2
    core = lax.rem(me, 2)
    far = 1 - core
    my_pair = me // 2
    mate_place = (my_kv, my_batch + 1 - 2 * core)
    pair_rows = pairs * per_device

    pre_copies = [
        pltpu.make_async_copy(pk_hbm, pk_raw, pre_sem.at[0]),
        pltpu.make_async_copy(pv_hbm, pv_raw, pre_sem.at[1]),
    ]
    for copy in pre_copies:
        copy.start()

    def suffix_copies(slot):
        return (
            pltpu.make_async_copy(sk_hbm.at[slot], sk.at[slot], suf_sem.at[0, slot]),
            pltpu.make_async_copy(sv_hbm.at[slot], sv.at[slot], suf_sem.at[1, slot]),
        )

    for slot in range(slots):
        for copy in suffix_copies(slot):
            copy.start()

    barrier = pltpu.get_barrier_semaphore()

    def peer(step):
        other = lax.rem(me + step, devices)
        return other, (other // batch_count, lax.rem(other, batch_count))

    def greet(step, carry):
        _, place = peer(step)
        pl.semaphore_signal(barrier, inc=1, device_id=place, device_id_type=MESH)
        return carry

    lax.fori_loop(1, devices, greet, 0)
    pl.semaphore_wait(barrier, devices - 1)

    def send(src, dst, send_sem, recv_sem, place):
        return pltpu.make_async_remote_copy(
            src_ref=src,
            dst_ref=dst,
            send_sem=send_sem,
            recv_sem=recv_sem,
            device_id=place,
            device_id_type=MESH,
        )

    my_heads = pl.ds(pl.multiple_of(my_kv * local, local), local)

    def query_start(step, carry):
        other, place = peer(2 * step)
        heads_there = pl.ds(pl.multiple_of(place[0] * local, local), local)
        send(
            q_ref.at[:, heads_there, :], qbuf.at[my_pair, core], q_send.at[other // 2],
            q_recv.at[my_pair], place,
        ).start()
        return carry

    lax.fori_loop(1, pairs, query_start, 0)
    own_forward = send(
        q_ref.at[:, my_heads, :], qbuf.at[my_pair, core], f_send.at[my_pair], f_recv.at[my_pair],
        mate_place,
    )
    own_forward.start()
    qbuf[my_pair, core] = q_ref[:, my_heads, :]

    for copy, raw, parted in zip(pre_copies, (pk_raw, pv_raw), (pk, pv)):
        copy.wait()
        spread[...] = raw[...].astype(F32)
        for k in range(kv_local):
            parted[k] = spread[pl.ds(k, prefix, stride=kv_local), :].astype(BF16)

    def forward(pair):
        return send(
            qbuf.at[pair, core], qbuf.at[pair, core], f_send.at[pair], f_recv.at[pair], mate_place
        )

    def query_wait(step, carry):
        other, place = peer(2 * step)
        pair = other // 2
        arrived = qbuf.at[pair, core]
        send(arrived, arrived, q_send.at[pair], q_recv.at[pair], place).wait()
        forward(pair).start()
        return carry

    lax.fori_loop(1, pairs, query_wait, 0)

    contract_last = (((1,), (1,)), ((), ()))

    def attend_prefix(side):
        qf[...] = qbuf[:, side].astype(F32).reshape(pair_rows * local, dim)
        for k in range(kv_local):
            parts = [qf[pl.ds(k * group + j, pair_rows, stride=local), :] for j in range(group)]
            q = jnp.concatenate(parts, axis=0).astype(BF16)
            scores = lax.dot_general(q, pk[k], contract_last, preferred_element_type=F32) * scale
            row_best = jnp.max(scores, axis=-1, keepdims=True)
            weights = jnp.exp(scores - row_best)
            row_total = jnp.sum(weights, axis=-1, keepdims=True)
            row_acc = jnp.dot(weights.astype(BF16), pv[k], preferred_element_type=F32)
            wide_best = jnp.broadcast_to(row_best, row_acc.shape)
            wide_total = jnp.broadcast_to(row_total, row_acc.shape)
            for j in range(group):
                there = pl.ds(k * group + j, pair_rows, stride=local)
                here = slice(j * pair_rows, (j + 1) * pair_rows)
                acc[side, there, :] = row_acc[here]
                best[side, there, :] = wide_best[here]
                total[side, there, :] = wide_total[here]

    attend_prefix(core)

    def forward_wait(pair, carry):
        arrived = qbuf.at[pair, far]
        send(arrived, arrived, f_send.at[pair], f_recv.at[pair], mate_place).wait()
        return carry

    lax.fori_loop(0, pairs, forward_wait, 0)
    attend_prefix(far)

    mate_copies = [
        send(table.at[far], there, m_send.at[n], m_recv.at[n], mate_place)
        for n, (table, there) in enumerate(
            ((acc, mate_acc), (best, mate_best), (total, mate_total))
        )
    ]
    for copy in mate_copies:
        copy.start()

    column = lax.broadcasted_iota(jnp.int32, (local, rows), 1)
    head_row = lax.broadcasted_iota(jnp.int32, (local, rows), 0)
    own_head = lax.rem(column, kv_local) == head_row // group
    lane = lax.broadcasted_iota(jnp.int32, (local, dim), 1)
    sub = lax.broadcasted_iota(jnp.int32, (local, dim), 0)
    half = per_device * local

    def attend_suffix(slot):
        for copy in suffix_copies(slot):
            copy.wait()
        sequence = seq_ref[slot]
        owner = sequence // per_device
        q = qbuf[owner // 2, lax.rem(owner, 2), lax.rem(sequence, per_device)]
        scores = lax.dot_general(q, sk[slot], contract_last, preferred_element_type=F32) * scale
        live = own_head & (column < len_ref[slot] * kv_local)
        scores = jnp.where(live, scores, FILL)
        row_best = jnp.max(scores, axis=-1, keepdims=True)
        weights = jnp.exp(scores - row_best)
        row_total = jnp.sum(weights, axis=-1, keepdims=True)
        suf_acc[slot] = jnp.dot(weights.astype(BF16), sv[slot], preferred_element_type=F32)
        suf_best[slot] = jnp.broadcast_to(row_best, (local, dim))
        suf_total[slot] = jnp.broadcast_to(row_total, (local, dim))

    def mark(stat, w, new_best, new_total):
        stat = jnp.where(lane == sub + w * local, new_best, stat)
        return jnp.where(lane == sub + half + w * local, new_total, stat)

    def fold_pair(pair, acc_out, stat_out):
        stat = jnp.zeros((local, dim), F32)
        for w in range(per_device):
            table = pl.ds(pl.multiple_of((pair * per_device + w) * local, local), local)
            first_best = best[core, table, :]
            second_best = mate_best[table, :]
            new_best = jnp.maximum(first_best, second_best)
            first = jnp.exp(first_best - new_best)
            second = jnp.exp(second_best - new_best)
            new_total = total[core, table, :] * first + mate_total[table, :] * second
            new_acc = acc[core, table, :] * first + mate_acc[table, :] * second
            acc_out[w] = new_acc.astype(BF16)
            stat = mark(stat, w, new_best, new_total)
        stat_out[...] = jnp.sum(stat, axis=0, keepdims=True)

    def prefix_sends(step):
        other, place = peer(2 * step)
        pair = other // 2
        return pair, (
            send(send_acc.at[pair], recv_acc.at[my_pair], r_send.at[0, pair], r_recv.at[0, my_pair], place),
            send(send_stat.at[pair], recv_stat.at[my_pair], r_send.at[1, pair], r_recv.at[1, my_pair], place),
        )

    def prefix_start(step, carry):
        pair, copies = prefix_sends(step)
        fold_pair(pair, send_acc.at[pair], send_stat.at[pair])
        for copy in copies:
            copy.start()
        return carry

    def prefix_wait(step, carry):
        other, place = peer(2 * step)
        pair = other // 2
        send(send_acc.at[pair], recv_acc.at[pair], r_send.at[0, pair], r_recv.at[0, pair], place).wait()
        send(send_stat.at[pair], recv_stat.at[pair], r_send.at[1, pair], r_recv.at[1, pair], place).wait()
        return carry

    def pick_slot(other, acc_out, stat_out):
        at = jnp.int32(0)
        hits = []
        for w in range(per_device):
            hit = jnp.int32(0)
            for slot in range(slots):
                same = (seq_ref[slot] == other * per_device + w).astype(jnp.int32)
                at = jnp.maximum(at, same * slot)
                hit = jnp.maximum(hit, same)
            hits.append(hit)
        stat = jnp.zeros((local, dim), F32)
        for w in range(per_device):
            stat = mark(
                stat, w, jnp.where(hits[w] > 0, suf_best[at], FILL),
                jnp.where(hits[w] > 0, suf_total[at], 0.0),
            )
        acc_out[...] = suf_acc[at].astype(BF16)
        stat_out[...] = jnp.sum(stat, axis=0, keepdims=True)

    def suffix_start(step, carry):
        other, place = peer(step)
        pick_slot(other, send_suf.at[other], send_sufstat.at[other])
        send(send_suf.at[other], recv_suf.at[me], u_send.at[0, other], u_recv.at[0, me], place).start()
        send(send_sufstat.at[other], recv_sufstat.at[me], u_send.at[1, other], u_recv.at[1, me], place).start()
        return carry

    def suffix_wait(step, carry):
        other, place = peer(step)
        send(send_suf.at[other], recv_suf.at[other], u_send.at[0, other], u_recv.at[0, other], place).wait()
        send(send_sufstat.at[other], recv_sufstat.at[other], u_send.at[1, other], u_recv.at[1, other], place).wait()
        return carry

    early = slots // 2
    for slot in range(early):
        attend_suffix(slot)
    for copy in mate_copies:
        copy.wait()
    lax.fori_loop(1, pairs, prefix_start, 0)
    fold_pair(my_pair, recv_acc.at[my_pair], recv_stat.at[my_pair])
    for slot in range(early, slots):
        attend_suffix(slot)
    lax.fori_loop(1, devices, suffix_start, 0)
    pick_slot(me, recv_suf.at[me], recv_sufstat.at[me])
    lax.fori_loop(1, pairs, prefix_wait, 0)

    def column_of(row, w):
        picked = jnp.where(lane == sub + w * local, row, 0.0)
        return jnp.sum(picked, axis=-1, keepdims=True)

    def widen(values):
        return jnp.concatenate([values, jnp.zeros((values.shape[0], dim - half), F32)], axis=1)

    chips = batch_count // 2
    states = []
    for g in range(kv_count):
        stats = recv_stat[g * chips : (g + 1) * chips, 0, :]
        top = jnp.max(stats[:, :half], axis=0, keepdims=True)
        factor = jnp.exp(stats[:, :half] - top)
        denominator = jnp.sum(stats[:, half : 2 * half] * factor, axis=0, keepdims=True)
        weight[:chips, 0, :] = widen(factor)

        def add_prefix(index, sums, g=g):
            row = weight[index]
            return tuple(
                sums[w] + column_of(row, w) * recv_acc[g * chips + index, w].astype(F32)
                for w in range(per_device)
            )

        zeros = tuple(jnp.zeros((local, dim), F32) for _ in range(per_device))
        states.append((top, denominator, lax.fori_loop(0, chips, add_prefix, zeros, unroll=4)))

    lax.fori_loop(1, devices, suffix_wait, 0)
    for g in range(kv_count):
        top, denominator, sums = states[g]
        stats = recv_sufstat[g * batch_count : (g + 1) * batch_count, 0, :]
        new_top = jnp.maximum(top, jnp.max(stats[:, :half], axis=0, keepdims=True))
        factor = jnp.exp(stats[:, :half] - new_top)
        kept = jnp.exp(top - new_top)
        denominator = denominator * kept + jnp.sum(
            stats[:, half : 2 * half] * factor, axis=0, keepdims=True
        )
        weight[:batch_count, 0, :] = widen(factor / denominator)
        kept_row = widen(kept / denominator)
        sums = tuple(sums[w] * column_of(kept_row, w) for w in range(per_device))

        def add_suffix(index, sums, g=g):
            row = weight[index]
            part = recv_suf[g * batch_count + index].astype(F32)
            return tuple(sums[w] + column_of(row, w) * part for w in range(per_device))

        sums = lax.fori_loop(0, batch_count, add_suffix, sums, unroll=4)
        for w in range(per_device):
            out_ref[w, g * local : (g + 1) * local, :] = sums[w].astype(BF16)


def solution(mesh):
    kv_count = mesh.shape["kv"]
    batch_count = mesh.shape["batch"]
    devices = kv_count * batch_count

    def step(queries, prefix_keys, prefix_values, suffix_keys, suffix_values, lengths, slot_sequence):
        per_device, heads, dim = queries.shape
        local = heads // kv_count
        prefix, kv_local, _ = prefix_keys.shape
        slots, suffix, _, _ = suffix_keys.shape
        group = local // kv_local
        sequences = devices * per_device
        flat = sequences * local
        vmem = pl.BlockSpec(memory_space=pltpu.VMEM)
        smem = pl.BlockSpec(memory_space=pltpu.SMEM)
        hbm = pl.BlockSpec(memory_space=pl.ANY)
        dma = pltpu.SemaphoreType.DMA
        return pl.pallas_call(
            functools.partial(kernel, kv_count, batch_count, group, dim ** (-0.5)),
            out_shape=jax.ShapeDtypeStruct(queries.shape, BF16),
            in_specs=[smem, smem, vmem, hbm, hbm, hbm, hbm],
            out_specs=vmem,
            scratch_shapes=[
                pltpu.VMEM((prefix * kv_local, dim), BF16),
                pltpu.VMEM((prefix * kv_local, dim), BF16),
                pltpu.VMEM((slots, suffix * kv_local, dim), BF16),
                pltpu.VMEM((slots, suffix * kv_local, dim), BF16),
                pltpu.VMEM((prefix * kv_local, dim), F32),
                pltpu.VMEM((kv_local, prefix, dim), BF16),
                pltpu.VMEM((kv_local, prefix, dim), BF16),
                pltpu.VMEM((devices // 2, 2, per_device, local, dim), BF16),
                pltpu.VMEM((flat // 2, dim), F32),
                pltpu.VMEM((2, flat // 2, dim), F32),
                pltpu.VMEM((2, flat // 2, dim), F32),
                pltpu.VMEM((2, flat // 2, dim), F32),
                pltpu.VMEM((flat // 2, dim), F32),
                pltpu.VMEM((flat // 2, dim), F32),
                pltpu.VMEM((flat // 2, dim), F32),
                pltpu.VMEM((slots, local, dim), F32),
                pltpu.VMEM((slots, local, dim), F32),
                pltpu.VMEM((slots, local, dim), F32),
                pltpu.VMEM((devices // 2, per_device, local, dim), BF16),
                pltpu.VMEM((devices // 2, 1, dim), F32),
                pltpu.VMEM((devices // 2, per_device, local, dim), BF16),
                pltpu.VMEM((devices // 2, 1, dim), F32),
                pltpu.VMEM((devices, local, dim), BF16),
                pltpu.VMEM((devices, 1, dim), F32),
                pltpu.VMEM((devices, local, dim), BF16),
                pltpu.VMEM((devices, 1, dim), F32),
                pltpu.VMEM((devices, 1, dim), F32),
                dma((2,)),
                dma((2, slots)),
                dma((devices // 2,)),
                dma((devices // 2,)),
                dma((devices // 2,)),
                dma((devices // 2,)),
                dma((3,)),
                dma((3,)),
                dma((2, devices // 2)),
                dma((2, devices // 2)),
                dma((2, devices)),
                dma((2, devices)),
            ],
            compiler_params=pltpu.CompilerParams(
                collective_id=0, has_side_effects=True, vmem_limit_bytes=60 * 1024 * 1024
            ),
        )(
            slot_sequence,
            lengths,
            queries,
            prefix_keys.reshape(prefix * kv_local, dim),
            prefix_values.reshape(prefix * kv_local, dim),
            suffix_keys.reshape(slots, suffix * kv_local, dim),
            suffix_values.reshape(slots, suffix * kv_local, dim),
        )

    return jax.shard_map(
        step,
        mesh=mesh,
        in_specs=(
            P(("kv", "batch"), None, None),
            P("batch", "kv", None),
            P("batch", "kv", None),
            P("batch", None, "kv", None),
            P("batch", None, "kv", None),
            P("batch"),
            P("batch"),
        ),
        out_specs=P(("kv", "batch"), None, None),
        check_vma=False,
    )
```

time: 35.5 us -> 32.9 us (0.927)
  Pallas kernels: 33.8 us -> 31.2 us
    pallas_call x1, Pallas kernels: 33.8 us -> 31.2 us  [step(): pl.pallas_call(functools.partial(kernel, kv_count, batch_count, group, di...]
where the time goes in v2:
time: 32.9 us; the launch traced here: 32.6 us
  Pallas kernels  31.2 us (95%)
  local copies, waits for them, and re-layouts  1.32 us (4%)
    pallas_call x1, Pallas kernels, step(): pl.pallas_call(functools.partial(kernel, kv_count, batch_count, group, di...  31.2 us
    unnamed x1, local copies, waits for them, and re-layouts  1.32 us

profile of v2, /device:TPU:0, one launch (start us, length us, event | category | flops | bytes accessed | tf_op | source)
XLA Modules:
  0.0 32.6 jit_solution(16090547981626853492)
XLA Ops:
  0.0 31.2 %shard_map.73 = bf16[2,32,128]{2,1,0:T(8,128)(2,1)} custom-call(s32[4]{0:T(128)} %seq_ref.1, s32[4]{0:T(128)} %len_ref.1, bf16[2,32,128]{2,1,0:T(8,128)(2,1)} %q_ref.1, bf16[2048,128]{1,0:T(8,128)(2,1)} %bitcast.6, bf16[2048,128]{1,0:T(8,128)(2,1)} %bitcast.7, bf16[4,8192,128]{2,1,0:T(8,128)(2,1)} %bitcast.4, bf16[4,8192,128]{2,1,0:T(8,128)(2,1)} %bitcast.5), custom_call_target="tpu_custom_call" | custom-call | tf_op jit(solution)/shard_map/pallas_call | solution.py:384
  31.2 1.3 %copy.9 = bf16[2,32,128]{2,1,0:T(8,128)(2,1)} copy(bf16[2,32,128]{2,1,0:T(8,128)(2,1)} %shard_map.73) | data formatting | bytes 32768

commit v3 on v2

--- a/solution.py
+++ b/solution.py
@@ -359,7 +359,7 @@
             part = recv_suf[g * batch_count + index].astype(F32)
             return tuple(sums[w] + column_of(row, w) * part for w in range(per_device))
 
-        sums = lax.fori_loop(0, batch_count, add_suffix, sums, unroll=4)
+        sums = lax.fori_loop(0, batch_count, add_suffix, sums, unroll=16)
         for w in range(per_device):
             out_ref[w, g * local : (g + 1) * local, :] = sums[w].astype(BF16)
 

time: 32.9 us -> 32.1 us (0.976)
  Pallas kernels: 31.2 us -> 30.5 us
    pallas_call x1, Pallas kernels: 31.2 us -> 30.5 us  [step(): pl.pallas_call(functools.partial(kernel, kv_count, batch_count, group, di...]
where the time goes in v3:
time: 32.1 us; the launch traced here: 31.8 us
  Pallas kernels  30.5 us (95%)
  local copies, waits for them, and re-layouts  1.32 us (4%)
    pallas_call x1, Pallas kernels, step(): pl.pallas_call(functools.partial(kernel, kv_count, batch_count, group, di...  30.5 us
    unnamed x1, local copies, waits for them, and re-layouts  1.32 us

profile of v3, /device:TPU:0, one launch (start us, length us, event | category | flops | bytes accessed | tf_op | source)
XLA Modules:
  0.0 31.8 jit_solution(14898105653451088651)
XLA Ops:
  0.0 30.5 %shard_map.73 = bf16[2,32,128]{2,1,0:T(8,128)(2,1)} custom-call(s32[4]{0:T(128)} %seq_ref.1, s32[4]{0:T(128)} %len_ref.1, bf16[2,32,128]{2,1,0:T(8,128)(2,1)} %q_ref.1, bf16[2048,128]{1,0:T(8,128)(2,1)} %bitcast.6, bf16[2048,128]{1,0:T(8,128)(2,1)} %bitcast.7, bf16[4,8192,128]{2,1,0:T(8,128)(2,1)} %bitcast.4, bf16[4,8192,128]{2,1,0:T(8,128)(2,1)} %bitcast.5), custom_call_target="tpu_custom_call" | custom-call | tf_op jit(solution)/shard_map/pallas_call | solution.py:384
  30.5 1.3 %copy.9 = bf16[2,32,128]{2,1,0:T(8,128)(2,1)} copy(bf16[2,32,128]{2,1,0:T(8,128)(2,1)} %shard_map.73) | data formatting | bytes 32768
